TPU v7x, 512 devices: a whole 4x4x16 slice. The times are simulated.
512 devices in a mesh: lat: 128 (over y, z, core), tok: 4 (over x).
Axes of the slice: x: 4, y: 4, z: 16, core: 2. Of those that a mesh axis runs over, the one named last changes fastest.
Arguments:
- inputs: bfloat16 [256, 3, 2304], P('lat', None, 'tok'), may hold values from -6 to 6
- targets: bfloat16 [256, 3, 2304], P('lat', None, 'tok'), may hold values from -6 to 6
- enc_weight: bfloat16 [3, 2304, 32768], P(None, 'tok', 'lat'), may hold values from -0.125 to 0.125
- enc_bias: float32 [3, 32768], P(None, 'lat'), may hold values from -3 to 3
- dec_weight: bfloat16 [6, 32768, 2304], P(None, 'lat', 'tok'), may hold values from -0.03125 to 0.03125
- counts: int32 [3, 128], P(None, 'lat'), may hold values from 32 to 256, as said below
Outputs:
- recon: bfloat16 [256, 3, 2304], P('lat', None, 'tok')
- dec_grad: bfloat16 [6, 32768, 2304], P(None, 'lat', 'tok')
- latent_grad: bfloat16 [256, 3, 32768], P('tok', None, 'lat')
Inputs may be any that keep to these rules, and one draw needn't show every extreme that they name: Latents 0 to counts[l, t] - 1 of layer l's tile on index t of lat are live, the rest dead; in every layer some tile has all 256 live.
All inputs are finite; a program needn't handle non-finite values.
Results may differ from a plain program's by a relative error of at most 0.0054.
Values may be sent and summed in bfloat16 or wider, within the bound.
A program may use at most 64 MiB of HBM per device.

v0:
```python
import jax
import jax.numpy as jnp
from jax import lax
from jax.sharding import Mesh
from jax.sharding import PartitionSpec as P

LAT = ("lat_0", "lat_1", "lat_2")


def joined_along(parts, dim):
    dims = list(parts.shape[1:])
    dims[dim] *= parts.shape[0]
    return jnp.moveaxis(parts, 0, dim).reshape(dims)


def all_blocks(array, axes, turns):
    parts = array
    for k in turns:
        parts = lax.all_gather(parts, axes[k])
    done = turns[::-1]
    back = [done.index(k) for k in range(len(axes))]
    parts = parts.transpose(*back, *range(len(axes), parts.ndim))
    return parts.reshape(-1, *array.shape)


def gathered_by_axis(array, axes, turns, dim):
    return joined_along(all_blocks(array, axes, turns), dim)


def copy_for_each(array, axis):
    copies = jnp.broadcast_to(array, (lax.axis_size(axis), *array.shape))
    return lax.all_to_all(copies, axis, split_axis=0, concat_axis=0, tiled=True)


def of_everyone(array, axis):
    return copy_for_each(array, axis).sum(axis=0)


def sum_in_order(parts, axes, turns):
    dims = [lax.axis_size(a) for a in axes]
    parts = parts.reshape(*dims, *parts.shape[1:])
    parts = parts.transpose(*turns, *range(len(axes), parts.ndim))
    parts = parts.reshape(-1, *parts.shape[len(axes) :])
    for k in turns:
        parts = lax.psum_scatter(parts, axes[k], scatter_dimension=0, tiled=True)
    return parts[0]


def in_blocks(array, dim, count):
    dims = array.shape
    parts = array.reshape(*dims[:dim], count, dims[dim] // count, *dims[dim + 1 :])
    return jnp.moveaxis(parts, dim, 0)


def sum_by_axis_2(array, axes, turns, dim):
    count = lax.axis_size(axes)
    return sum_in_order(in_blocks(array, dim, count), axes, turns)


def sent_and_summed(array, axis, dim):
    parts = in_blocks(array, dim, lax.axis_size(axis))
    arrived = lax.all_to_all(parts, axis, split_axis=0, concat_axis=0, tiled=True)
    return arrived.sum(axis=0)


def block_index(source, target, layers):
    return source * layers - source * (source - 1) // 2 + (target - source)


def forward_tile(tile_values, weight):
    return jnp.dot(tile_values, weight, preferred_element_type=jnp.float32)


def backward_tile(error_rows, weight):
    contract = (((1,), (1,)), ((), ()))
    return lax.dot_general(error_rows, weight, contract, preferred_element_type=jnp.float32)


def weight_tile(tile_values, error_rows):
    contract = (((0,), (0,)), ((), ()))
    return lax.dot_general(tile_values, error_rows, contract, preferred_element_type=jnp.float32)


def local(inputs, targets, enc_weight, enc_bias, dec_weight, counts):
    layers = inputs.shape[1]
    tile_width = enc_weight.shape[2]
    live_mask = lax.broadcasted_iota(jnp.int32, (layers, tile_width), 1) < counts
    gathered = gathered_by_axis(inputs, LAT, (0, 1, 2), 0)
    partial_pre = jnp.einsum(
        "tld,ldk->tlk", gathered, enc_weight, preferred_element_type=jnp.float32
    )
    preact = of_everyone(partial_pre, "tok")
    preact = preact + enc_bias[None]
    latents = jnp.where(live_mask[None], jnp.maximum(preact, 0.0), 0.0).astype(jnp.bfloat16)
    picked = latents
    stacked = []
    for decode_target in range(layers):
        summed = forward_tile(picked[:, 0, :], dec_weight[block_index(0, decode_target, layers)])
        for decode_source in range(1, decode_target + 1):
            summed = summed + forward_tile(
                picked[:, decode_source, :],
                dec_weight[block_index(decode_source, decode_target, layers)],
            )
        stacked.append(summed)
    full_recon = sum_by_axis_2(jnp.stack(stacked, axis=1), LAT, (2, 1, 0), 0)
    own_errors = (full_recon - targets.astype(jnp.float32)).astype(jnp.bfloat16)
    errors = gathered_by_axis(own_errors, LAT, (0, 1, 2), 0)
    recon = full_recon.astype(jnp.bfloat16)
    grads = []
    for source in range(layers):
        for target in range(source, layers):
            grads.append(
                weight_tile(latents[:, source, :], errors[:, target, :]).astype(jnp.bfloat16)
            )
    dec_grad = jnp.stack(grads, axis=0)
    picked = errors
    stacked = []
    for source in range(layers):
        summed = backward_tile(
            picked[:, source, :], dec_weight[block_index(source, source, layers)]
        )
        for target in range(source + 1, layers):
            summed = summed + backward_tile(
                picked[:, target, :], dec_weight[block_index(source, target, layers)]
            )
        stacked.append(summed)
    latent_sum = sent_and_summed(jnp.stack(stacked, axis=1), "tok", 0)
    latent_grad = jnp.where(live_mask[None], latent_sum, 0.0).astype(jnp.bfloat16)
    return (recon, dec_grad, latent_grad)


def solution(mesh):
    split = Mesh(
        mesh.devices.reshape(4, 16, 2, mesh.shape["tok"]), ("lat_0", "lat_1", "lat_2", "tok")
    )
    in_specs = (
        P(LAT, None, "tok"),
        P(LAT, None, "tok"),
        P(None, "tok", LAT),
        P(None, LAT),
        P(None, LAT, "tok"),
        P(None, LAT),
    )
    out_specs = (P(LAT, None, "tok"), P(None, LAT, "tok"), P("tok", None, LAT))
    return jax.shard_map(local, mesh=split, in_specs=in_specs, out_specs=out_specs, check_vma=False)
```

profile of v0, /device:TPU:1, one launch (start us, length us, event | category | flops | bytes accessed | tf_op | source)
XLA Modules:
  0.0 411.3 jit_solution(12321016868124942372)
XLA Ops:
  7.2 0.8 copy.34
  8.0 10.4 %all-gather = bf16[8,3,576]{2,1,0:T(4,128)(2,1)S(1)} all-gather(bf16[2,3,576]{2,1,0:T(4,128)(2,1)S(1)} %copy.34), channel_id=2, replica_groups=mesh['lat_0'=4,'lat_1'=16,'lat_2'=2,'tok'=4] {'lat_0'}, dimensions={0}, use_global_device_ids=true | all-gather | bytes 34560 | tf_op jit(solution)/shard_map/all_gather | solution.py:19
  18.4 30.8 %all-gather.1 = bf16[64,2,3,576]{3,1,2,0:T(2,128)(2,1)S(1)} all-gather(bf16[4,2,3,576]{3,1,2,0:T(2,128)(2,1)S(1)} %copy.35), channel_id=3, replica_groups=mesh['lat_0'=4,'lat_1'=16,'lat_2'=2,'tok'=4] {'lat_1'}, dimensions={0}, use_global_device_ids=true | all-gather | bytes 470016 | tf_op jit(solution)/shard_map/all_gather | solution.py:19
  49.1 0.2 copy.36
  49.3 12.9 %all-gather.2 = bf16[32,4,2,3,576]{4,1,3,2,0:T(4,128)(2,1)S(1)} all-gather(bf16[16,4,2,3,576]{4,1,3,2,0:T(4,128)(2,1)S(1)} %copy.36), channel_id=4, replica_groups=mesh['lat_0'=4,'lat_1'=16,'lat_2'=2,'tok'=4] {'lat_2'}, dimensions={0}, use_global_device_ids=true | all-gather | bytes 1327104 | tf_op jit(solution)/shard_map/all_gather | solution.py:19
  62.3 0.1 copy.37
  62.4 0.9 copy.38
  63.3 0.8 reshape_reshape.7
  64.1 0.5 convolution_bitcast_fusion
  64.6 0.3 copy.40
  64.9 2.0 broadcast_in_dim.29
  66.8 4.8 %all-to-all-start = ((f32[4,256,3,256]{3,1,2,0:T(8,128)}), f32[4,256,3,256]{3,1,2,0:T(8,128)}, u32[]{:S(2)}, u32[]{:S(2)}) async-start(f32[4,256,3,256]{3,1,2,0:T(8,128)} %broadcast_in_dim.29), calls=%async_computation | async-start | bytes 6291456 | tf_op jit(solution)/shard_map/all_to_all | solution.py:32
  71.7 0.1 iota_compare_fusion
  71.8 37.2 %all-to-all-done = f32[4,256,3,256]{3,1,2,0:T(8,128)} async-done(((f32[4,256,3,256]{3,1,2,0:T(8,128)}), f32[4,256,3,256]{3,1,2,0:T(8,128)}, u32[]{:S(2)}, u32[]{:S(2)}) %all-to-all-start) | async-done | bytes 3145760 | tf_op jit(solution)/shard_map/all_to_all | solution.py:32
  109.0 3.1 reduce_sum.18
  112.1 1.2 select_convert_fusion
  113.3 0.3 fusion.23
  113.6 1.1 fusion.29
  114.7 0.3 convolution_add_fusion.1
  114.9 1.1 convolution_add_fusion
  116.0 2.1 copy.43
  118.2 2.3 stack.42
  120.5 2.0 copy.45
  122.5 2.2 convolution_add_fusion.2
  124.6 2.2 copy.42
  126.8 2.3 stack.41
  129.1 2.0 copy.44
  131.2 0.3 convolution_bitcast_fusion.1
  131.5 1.4 maximum_bitcast_fusion
  132.9 2.3 copy.46
  135.3 1.3 dynamic-slice
  137.2 35.7 %all-reduce.6.cloned.1.call-done = f32[128,2,3,576]{3,1,2,0:T(2,128)} async-done(((f32[128,2,3,576]{3,1,2,0:T(2,128)}), f32[128,2,3,576]{3,1,2,0:T(2,128)}) %all-reduce.6.cloned.1.call-update) | async-done | bytes 1769488
  172.9 2.5 constant_dynamic-slice_fusion.1
  175.4 1.3 dynamic-slice.2
  176.7 1.3 dynamic-slice.4
  178.6 126.7 %all-reduce.8.cloned.1.call-done = f32[64,2,3,576]{3,1,2,0:T(2,128)} async-done(((f32[64,2,3,576]{3,1,2,0:T(2,128)}), f32[64,2,3,576]{3,1,2,0:T(2,128)}) %all-reduce.8.cloned.1.call-update) | async-done | bytes 884752
  305.3 0.8 constant_dynamic-slice_fusion
  306.1 14.1 %all-reduce.2 = f32[4,2,3,576]{3,1,2,0:T(2,128)S(1)} all-reduce(f32[4,2,3,576]{3,1,2,0:T(2,128)S(1)} %constant_dynamic-slice_fusion), channel_id=10, replica_groups=mesh['lat_0'=4,'lat_1'=16,'lat_2'=2,'tok'=4] {'lat_0'}, use_global_device_ids=true, to_apply=%region_3.4.clone | all-reduce | flops 13824 | bytes 110592
  320.3 0.7 subtract_convert_fusion
  320.9 9.0 %all-gather.3 = bf16[8,3,576]{2,1,0:T(4,128)(2,1)S(1)} all-gather(bf16[2,3,576]{2,1,0:T(4,128)(2,1)S(1)} %copy.47), channel_id=5, replica_groups=mesh['lat_0'=4,'lat_1'=16,'lat_2'=2,'tok'=4] {'lat_0'}, dimensions={0}, use_global_device_ids=true | all-gather | bytes 34560 | tf_op jit(solution)/shard_map/all_gather | solution.py:19
  330.0 23.1 %all-gather.4 = bf16[64,2,3,576]{3,1,2,0:T(2,128)(2,1)S(1)} all-gather(bf16[4,2,3,576]{3,1,2,0:T(2,128)(2,1)S(1)} %copy.48), channel_id=6, replica_groups=mesh['lat_0'=4,'lat_1'=16,'lat_2'=2,'tok'=4] {'lat_1'}, dimensions={0}, use_global_device_ids=true | all-gather | bytes 470016 | tf_op jit(solution)/shard_map/all_gather | solution.py:19
  353.1 0.2 copy.49
  353.3 26.7 %all-gather.5 = bf16[32,4,2,3,576]{4,1,3,2,0:T(4,128)(2,1)S(1)} all-gather(bf16[16,4,2,3,576]{4,1,3,2,0:T(4,128)(2,1)S(1)} %copy.49), channel_id=7, replica_groups=mesh['lat_0'=4,'lat_1'=16,'lat_2'=2,'tok'=4] {'lat_2'}, dimensions={0}, use_global_device_ids=true | all-gather | bytes 1327104 | tf_op jit(solution)/shard_map/all_gather | solution.py:19
  380.0 0.1 copy.50
  380.1 0.9 copy.51
  381.0 0.8 reshape_reshape.8
  381.8 0.3 fusion.1
  382.1 1.4 fusion.25
  383.5 0.3 fusion.31
  383.8 0.3 fusion.3
  384.1 0.3 fusion.5
  384.4 0.3 fusion.7
  384.7 1.2 copy-done.8
  385.9 0.3 convolution_bitcast_fusion.2
  386.2 0.3 convolution_add_fusion.3
  386.4 0.3 convolution_add_fusion.5
  386.7 0.3 convolution_add_fusion.4
  387.0 1.0 copy.52
  388.0 4.0 all-to-all-start.1
  392.0 1.2 fusion.51
  393.2 1.0 fusion.9
  394.2 1.0 fusion.11
  395.2 8.5 %all-to-all-done.1 = f32[4,64,3,256]{3,1,2,0:T(8,128)S(1)} async-done(((f32[4,64,3,256]{3,1,2,0:T(8,128)}), f32[4,64,3,256]{3,1,2,0:T(8,128)S(1)}, u32[]{:S(2)}, u32[]{:S(2)}) %all-to-all-start.1) | async-done | bytes 786464 | tf_op jit(solution)/shard_map/all_to_all | solution.py:62
  403.8 0.7 select_convert_fusion.1
  (30 shorter events, 0.4 us)
Async XLA Ops:
  7.2 56.9 %copy-start = (bf16[3,576,256]{2,1,0:T(8,128)(2,1)S(1)}, bf16[3,576,256]{2,1,0:T(8,128)(2,1)}, u32[]{:S(2)}) copy-start(bf16[3,576,256]{2,1,0:T(8,128)(2,1)} %param.8) | copy-start | bytes 2654212
  66.8 4.8 %copy-start.7 = (s32[3,1]{0,1:T(1,128)S(1)}, s32[3,1]{0,1:T(1,128)}, u32[]{:S(2)}) copy-start(s32[3,1]{0,1:T(1,128)} %param.11) | copy-start | bytes 40
  66.8 42.1 %all-to-all-start = ((f32[4,256,3,256]{3,1,2,0:T(8,128)}), f32[4,256,3,256]{3,1,2,0:T(8,128)}, u32[]{:S(2)}, u32[]{:S(2)}) async-start(f32[4,256,3,256]{3,1,2,0:T(8,128)} %broadcast_in_dim.29), calls=%async_computation | async-start | bytes 6291456 | tf_op jit(solution)/shard_map/all_to_all | solution.py:32
  71.6 101.3 %all-reduce.6.cloned.1.call-start = ((), (), s32[]{:S(2)}) async-start(), calls=%async_computation.2 | async-start | bytes 3932160
  71.8 40.3 %copy-start.6 = (f32[3,256]{1,0:T(4,128)S(1)}, f32[3,256]{1,0:T(4,128)}, u32[]{:S(2)}) copy-start(f32[3,256]{1,0:T(4,128)} %param.9) | copy-start | bytes 9220
  71.8 41.5 %copy-start.1 = (bf16[6,256,576]{1,2,0:T(8,128)(2,1)S(1)}, bf16[6,256,576]{1,2,0:T(8,128)(2,1)}, u32[]{:S(2)}) copy-start(bf16[6,256,576]{1,2,0:T(8,128)(2,1)} %param.10) | copy-start | bytes 5308420
  113.3 9.2 %copy-start.3 = (bf16[256,3,256]{2,0,1:T(8,128)(2,1)}, bf16[256,3,256]{2,0,1:T(8,128)(2,1)S(1)}, u32[]{:S(2)}) copy-start(bf16[256,3,256]{2,0,1:T(8,128)(2,1)S(1)} %select_convert_fusion) | copy-start | bytes 1179652
  124.6 6.5 %slice-start = ((bf16[256,3,256]{2,0,1:T(8,128)(2,1)}), bf16[256,1,256]{2,0,1:T(8,128)(2,1)S(1)}, s32[]{:S(2)}) async-start(bf16[256,3,256]{2,0,1:T(8,128)(2,1)} %copy-done.3), calls=%async_computation.4 | async-start | bytes 262144 | tf_op jit(solution)/shard_map/slice | solution.py:98
  135.2 185.0 %copy-start.5 = (bf16[2,3,576]{2,0,1:T(2,128)(2,1)S(1)}, bf16[2,3,576]{2,0,1:T(2,128)(2,1)}, u32[]{:S(2)}) copy-start(bf16[2,3,576]{2,0,1:T(2,128)(2,1)} %param.7) | copy-start | bytes 20740
  135.2 170.1 %all-reduce.8.cloned.1.call-start = ((), (), s32[]{:S(2)}) async-start(), calls=%async_computation.3 | async-start | bytes 1966080
  380.1 1.7 copy-start.4
  381.8 1.8 copy-start.2
  384.7 1.2 copy-start.8
  388.0 15.7 %all-to-all-start.1 = ((f32[4,64,3,256]{3,1,2,0:T(8,128)}), f32[4,64,3,256]{3,1,2,0:T(8,128)S(1)}, u32[]{:S(2)}, u32[]{:S(2)}) async-start(f32[4,64,3,256]{3,1,2,0:T(8,128)} %copy.52), calls=%async_computation.1 | async-start | bytes 1572864 | tf_op jit(solution)/shard_map/all_to_all | solution.py:62
Sparse Core Ops, SparseCore 0:
  135.3 37.5 all-reduce.5
  175.8 129.4 all-reduce.7
where the time goes:
time: 412 us; the launch traced here: 411 us
  waiting for transfers between devices  208 us (50%)
  blocking collectives  127 us (31%)
  local copies, waits for them, and re-layouts  32.8 us (8%)
  between operations  15.7 us (4%)
  matrix products  11.6 us (3%)
  starting transfers between devices  8.84 us (2%)
  other arithmetic  7.22 us (2%)
    unnamed x4, waiting for transfers between devices  162 us
    all_gather x6, blocking collectives, all_blocks(): parts = lax.all_gather(parts, axes[k])  113 us
    all_to_all x1, waiting for transfers between devices, copy_for_each(): return lax.all_to_all(copies, axis, split_axis=0, concat_axis=0, tiled=True)  37.2 us
    unnamed x1, blocking collectives  14.1 us
    unnamed x24, local copies, waits for them, and re-layouts  9.14 us
    another operation x4, local copies, waits for them, and re-layouts, local(): full_recon = sum_by_axis_2(jnp.stack(stacked, axis=1), LAT, (2, 1, 0), 0)  8.59 us
    all_to_all x1, waiting for transfers between devices, sent_and_summed(): lax.all_to_all(parts, axis, split_axis=0, concat_axis=0, tiled=True)  8.47 us
  transfers between devices with their start and end apart: 4, of which 4 were waited for; matrix products, arithmetic and copies ran while one was open for 2% of the time, Pallas kernels for 0%

commit v1 on v0

v1 whole, which is shorter than its diff:
```python
import functools

import jax
import jax.numpy as jnp
from jax import lax
from jax.experimental import pallas as pl
from jax.experimental.pallas import tpu as pltpu
from jax.sharding import PartitionSpec as P

MESH = pl.DeviceIdType.MESH
F32 = jnp.float32
BF16 = jnp.bfloat16

STEPS = {
    "a1": 9.0, "a2": 13.0, "a3": 15.0, "b1": 19.0, "b2": 23.0, "c1": 25.0,
    "c2": 29.0, "c3": 38.0, "d1": 47.0, "d2": 51.0, "d3": 53.0,
}
SPACING = 1.8


def block_index(source, target, layers):
    return source * layers - source * (source - 1) // 2 + (target - source)


def dot_nn(a, b):
    return lax.dot_general(a, b, (((1,), (0,)), ((), ())), preferred_element_type=F32)


def dot_nt(a, b):
    return lax.dot_general(a, b, (((1,), (1,)), ((), ())), preferred_element_type=F32)


def dot_tn(a, b):
    return lax.dot_general(a, b, (((0,), (0,)), ((), ())), preferred_element_type=F32)


def kernel(
    sizes,
    in_hbm, tg_hbm, ew_hbm, bias_hbm, dw_hbm, cnt_hbm,
    recon_ref, dg_ref, lg_ref,
    own_in, tg, ew, bias, cnt, dw,
    zin, ga, pf, pp, pr, lt, rf, cr, ys, yr, zf, zs, zr, own_er, ez, ge, ef, es, er,
    load_sem, z_send, z_recv, y_send, y_recv, x_send, x_recv, c_send, c_recv,
):
    ny, nz, nx = sizes
    layers, pair, width = own_in.shape
    tile = ew.shape[2]
    rows = nz * pair
    tokens = 2 * ny * rows
    lat = lax.axis_index("lat")
    x = lax.axis_index("tok")
    c = lax.rem(lat, 2)
    z = lax.rem(lax.div(lat, 2), nz)
    y = lax.div(lat, 2 * nz)
    mate = 1 - c

    def device(y_at, z_at, c_at, x_at):
        return {"lat": (y_at * nz + z_at) * 2 + c_at, "tok": x_at}

    def z_peer(k):
        return device(y, k, c, x)

    def y_peer(k):
        return device(k, z, c, x)

    def x_peer(k):
        return device(y, z, c, k)

    loads = [
        pltpu.make_async_copy(src, dst, load_sem.at[i])
        for i, (src, dst) in enumerate(
            ((in_hbm, own_in), (tg_hbm, tg), (bias_hbm, bias), (cnt_hbm, cnt), (ew_hbm, ew), (dw_hbm, dw))
        )
    ]
    for load in loads:
        load.start()

    barrier = pltpu.get_barrier_semaphore()

    def greet(count, me, peer):
        @pl.loop(1, count)
        def _(k):
            pl.semaphore_signal(
                barrier, inc=1, device_id=peer(lax.rem(me + k, count)), device_id_type=MESH
            )

    greet(nz, z, z_peer)
    greet(ny, y, y_peer)
    greet(nx, x, x_peer)
    pl.semaphore_signal(barrier, inc=1, device_id=device(y, z, mate, x), device_id_type=MESH)
    pl.semaphore_wait(barrier, nz + ny + nx - 2)

    def remote(src, dst, send, recv, to):
        return pltpu.make_async_remote_copy(
            src_ref=src, dst_ref=dst, send_sem=send, recv_sem=recv, device_id=to, device_id_type=MESH
        )

    def exchange(phase, l, count, me, peer, send, recv, part, slot):
        half = count // 2

        def start():
            @pl.loop(0, count - 1)
            def _(k):
                far = half - lax.div(k + 1, 2)
                sign = 1 - 2 * lax.rem(k + 1, 2)
                to = lax.rem(me + count + sign * far, count)
                remote(part(to), slot(me), send.at[phase, l, to], recv.at[phase, l, me], peer(to)).start()

        def arrive():
            @pl.loop(1, count)
            def _(k):
                k = lax.rem(me + k, count)
                remote(part(k), slot(k), send.at[phase, l, k], recv.at[phase, l, k], peer(k)).wait_recv()

        def drain():
            @pl.loop(1, count)
            def _(k):
                k = lax.rem(me + k, count)
                remote(part(k), slot(k), send.at[phase, l, k], recv.at[phase, l, k], peer(k)).wait_send()

        return start, arrive, drain

    def z_exchange(phase, l, part, slot):
        return exchange(phase, l, nz, z, z_peer, z_send, z_recv, part, slot)

    def y_exchange(phase, l, part, slot):
        return exchange(phase, l, ny, y, y_peer, y_send, y_recv, part, slot)

    def x_exchange(phase, l, part, slot):
        return exchange(phase, l, nx, x, x_peer, x_send, x_recv, part, slot)

    def swap(phase, l, src, dst):
        return remote(src, dst, c_send.at[phase, l], c_recv.at[phase, l], device(y, z, mate, x))

    every = range(layers)
    a1 = [z_exchange(0, l, lambda k, l=l: own_in.at[l], lambda k, l=l: zin.at[l, k]) for l in every]
    c3 = [z_exchange(1, l, lambda k, l=l: zs.at[l, k], lambda k, l=l: zr.at[l, k]) for l in every]
    d1 = [z_exchange(2, l, lambda k, l=l: own_er.at[l], lambda k, l=l: ez.at[l, k]) for l in every]
    a2 = [y_exchange(0, l, lambda k, l=l: ga.at[l, c, y], lambda k, l=l: ga.at[l, c, k]) for l in every]
    c2 = [y_exchange(1, l, lambda k, l=l: ys.at[l, k], lambda k, l=l: yr.at[l, k]) for l in every]
    d2 = [y_exchange(2, l, lambda k, l=l: ge.at[l, c, y], lambda k, l=l: ge.at[l, c, k]) for l in every]
    b1 = [x_exchange(0, l, lambda k, l=l: pp.at[l, :, k], lambda k, l=l: pr.at[l, k]) for l in every]
    b2 = [x_exchange(1, l, lambda k, l=l: lt.at[l, :, x], lambda k, l=l: lt.at[l, :, k]) for l in every]
    e1 = [x_exchange(2, l, lambda k, l=l: es.at[l, :, k], lambda k, l=l: er.at[l, k]) for l in every]
    a3 = [swap(0, l, ga.at[l, c], ga.at[l, c]) for l in every]
    a3_in = [swap(0, l, ga.at[l, mate], ga.at[l, mate]) for l in every]
    c1 = [swap(1, l, rf.at[l, mate], cr.at[l]) for l in every]
    d3 = [swap(2, l, ge.at[l, c], ge.at[l, c]) for l in every]
    d3_in = [swap(2, l, ge.at[l, mate], ge.at[l, mate]) for l in every]

    loads[0].wait()
    for l in every:
        a1[l][0]()
    for l in every:
        zin[l, z] = own_in[l]
    for load in loads[1:]:
        load.wait()

    def live(l):
        return lax.broadcasted_iota(jnp.int32, (1, tile), 1) < cnt[0:1, l : l + 1]

    def joined(blocks):
        return blocks.astype(F32).reshape(rows, width).astype(BF16)

    def step_a1(l):
        a1[l][1]()
        ga[l, c, y] = joined(zin[l])
        a2[l][0]()

    def step_a2(l):
        a2[l][1]()
        a3[l].start()

    def step_a3(l):
        a3_in[l].wait_recv()
        partial = dot_nn(ga[l].reshape(tokens, width), ew[l]).reshape(2, ny, rows, tile)
        pf[l] = partial
        pp[l] = partial.astype(BF16)
        b1[l][0]()

    def step_b1(l):
        b1[l][1]()
        summed = pf[l, :, x]
        for k in range(1, nx):
            summed = summed + pr[l, lax.rem(x + k, nx)].astype(F32)
        summed = summed + bias[l : l + 1, :].reshape(1, 1, tile)
        alive = live(l).reshape(1, 1, tile)
        lt[l, :, x] = jnp.where(alive, jnp.maximum(summed, 0.0), 0.0).astype(BF16)
        b2[l][0]()

    def step_b2(m):
        b2[m][1]()
        total = None
        for l in range(m + 1):
            term = dot_nt(lt[l].reshape(tokens, tile), dw[block_index(l, m, layers)])
            total = term if total is None else total + term
        rf[m] = total.reshape(2, ny, rows, width)
        c1[m].start()

    def step_c1(m):
        c1[m].wait_recv()
        ys[m] = (rf[m, c] + cr[m]).astype(BF16)
        c2[m][0]()

    def step_c2(m):
        c2[m][1]()
        summed = rf[m, c, y] + cr[m, y]
        for k in range(1, ny):
            summed = summed + yr[m, lax.rem(y + k, ny)].astype(F32)
        blocks = summed.reshape(nz, pair, width)
        zf[m] = blocks
        zs[m] = blocks.astype(BF16)
        c3[m][0]()

    def step_c3(m):
        c3[m][1]()
        full = zf[m, z]
        for k in range(1, nz):
            full = full + zr[m, lax.rem(z + k, nz)].astype(F32)
        errors = (full - tg[m].astype(F32)).astype(BF16)
        own_er[m] = errors
        d1[m][0]()
        ez[m, z] = errors
        recon_ref[m] = full.astype(BF16)

    def step_d1(m):
        d1[m][1]()
        ge[m, c, y] = joined(ez[m])
        d2[m][0]()

    def step_d2(m):
        d2[m][1]()
        d3[m].start()

    def step_d3(m):
        d3_in[m].wait_recv()
        rows_of = ge[m].reshape(tokens, width)
        for l in range(m + 1):
            term = dot_nn(rows_of, dw[block_index(l, m, layers)]).reshape(2, ny, rows, tile)
            term = term if l == m else ef[l] + term
            ef[l] = term
            if m == layers - 1:
                es[l] = term.astype(BF16)
                e1[l][0]()
        for l in range(m + 1):
            dg_ref[block_index(l, m, layers)] = dot_tn(rows_of, lt[l].reshape(tokens, tile)).astype(BF16)

    acts = dict(
        a1=step_a1, a2=step_a2, a3=step_a3, b1=step_b1, b2=step_b2, c1=step_c1,
        c2=step_c2, c3=step_c3, d1=step_d1, d2=step_d2, d3=step_d3,
    )
    order = sorted((at + SPACING * l, name, l) for name, at in STEPS.items() for l in every)
    for _, name, l in order:
        acts[name](l)

    for l in every:
        e1[l][1]()
        summed = ef[l, :, x]
        for k in range(1, nx):
            summed = summed + er[l, lax.rem(x + k, nx)].astype(F32)
        lg_ref[l] = jnp.where(live(l).reshape(1, 1, tile), summed, 0.0).astype(BF16)

    for group in (a1, a2, b1, b2, c2, c3, d1, d2, e1):
        for l in every:
            group[l][2]()
    for group in (a3, c1, d3):
        for l in every:
            group[l].wait_send()


def build(mesh, sizes):
    ny, nz, nx = sizes

    def local(inputs, targets, enc_weight, enc_bias, dec_weight, counts):
        pair, layers, width = inputs.shape
        tile = enc_weight.shape[2]
        blocks = dec_weight.shape[0]
        rows = nz * pair
        in_hbm = pl.BlockSpec(memory_space=pltpu.HBM)
        in_vmem = pl.BlockSpec(memory_space=pltpu.VMEM)

        def vmem(*shape, dtype=BF16):
            return pltpu.VMEM(shape, dtype)

        def sems(*shape):
            return pltpu.SemaphoreType.DMA(shape)

        recon, dec_grad, latent_grad = pl.pallas_call(
            functools.partial(kernel, sizes),
            out_shape=(
                jax.ShapeDtypeStruct((layers, pair, width), BF16),
                jax.ShapeDtypeStruct((blocks, width, tile), BF16),
                jax.ShapeDtypeStruct((layers, 2, rows, tile), BF16),
            ),
            in_specs=[in_hbm] * 6,
            out_specs=(in_vmem, in_vmem, in_vmem),
            scratch_shapes=[
                vmem(layers, pair, width),
                vmem(layers, pair, width),
                vmem(layers, width, tile),
                vmem(layers, tile, dtype=F32),
                vmem(1, layers, dtype=jnp.int32),
                vmem(blocks, width, tile),
                vmem(layers, nz, pair, width),
                vmem(layers, 2, ny, rows, width),
                vmem(layers, 2, ny, rows, tile, dtype=F32),
                vmem(layers, 2, ny, rows, tile),
                vmem(layers, nx, 2, rows, tile),
                vmem(layers, 2, ny, rows, tile),
                vmem(layers, 2, ny, rows, width, dtype=F32),
                vmem(layers, ny, rows, width, dtype=F32),
                vmem(layers, ny, rows, width),
                vmem(layers, ny, rows, width),
                vmem(layers, nz, pair, width, dtype=F32),
                vmem(layers, nz, pair, width),
                vmem(layers, nz, pair, width),
                vmem(layers, pair, width),
                vmem(layers, nz, pair, width),
                vmem(layers, 2, ny, rows, width),
                vmem(layers, 2, ny, rows, tile, dtype=F32),
                vmem(layers, 2, ny, rows, tile),
                vmem(layers, nx, 2, rows, tile),
                sems(6),
                sems(3, layers, nz), sems(3, layers, nz),
                sems(3, layers, ny), sems(3, layers, ny),
                sems(3, layers, nx), sems(3, layers, nx),
                sems(3, layers), sems(3, layers),
            ],
            compiler_params=pltpu.CompilerParams(
                collective_id=0, has_side_effects=True, vmem_limit_bytes=48 * 1024 * 1024
            ),
        )(
            inputs.transpose(1, 0, 2),
            targets.transpose(1, 0, 2),
            enc_weight,
            enc_bias,
            dec_weight.transpose(0, 2, 1),
            counts.T,
        )
        latent_grad = latent_grad.reshape(layers, 2, nz, pair, tile).transpose(2, 1, 3, 0, 4)
        return (
            recon.transpose(1, 0, 2),
            dec_grad.transpose(0, 2, 1),
            latent_grad.reshape(2 * rows, layers, tile),
        )

    in_specs = (
        P("lat", None, "tok"),
        P("lat", None, "tok"),
        P(None, "tok", "lat"),
        P(None, "lat"),
        P(None, "lat", "tok"),
        P(None, "lat"),
    )
    out_specs = (P("lat", None, "tok"), P(None, "lat", "tok"), P("tok", None, "lat"))
    return jax.shard_map(local, mesh=mesh, in_specs=in_specs, out_specs=out_specs, check_vma=False)


def solution(mesh):
    nx = mesh.shape["tok"]
    return build(mesh, (4, mesh.shape["lat"] // 8, nx))
```

time: 412 us -> 90.8 us (0.22)
  waiting for transfers between devices: 208 us -> 0 us
  blocking collectives: 127 us -> 0 us
  Pallas kernels: 0 us -> 81.8 us
  local copies, waits for them, and re-layouts: 32.8 us -> 7.97 us
  between operations: 15.7 us -> 0.67 us
  matrix products: 11.6 us -> 0 us
  starting transfers between devices: 8.84 us -> 0 us
  other arithmetic: 7.22 us -> 0 us
    unnamed x4 -> x0, waiting for transfers between devices: 162 us -> none
    all_gather x6 -> x0, blocking collectives: 113 us -> none  [all_blocks(): parts = lax.all_gather(parts, axes[k])]
    pallas_call x0 -> x1, Pallas kernels: none -> 81.8 us  [local(): pl.pallas_call(functools.partial(kernel, sizes), out_shape=(jax.ShapeDtyp...]
    all_to_all x2 -> x0, waiting for transfers between devices: 45.7 us -> none  [the longest x1 37.2 us: copy_for_each(): return lax.all_to_all(copies, axis, split_axis=0, concat_axis=0, tiled=True)]
    unnamed x1 -> x0, blocking collectives: 14.1 us -> none
    dot_general x19 -> x0, matrix products: 11.6 us -> none  [the longest x6 5.18 us: forward_tile(): return jnp.dot(tile_values, weight, preferred_element_type=jnp.float32)]
    another operation x7 -> x0, local copies, waits for them, and re-layouts: 11.1 us -> none  [the longest x4 8.59 us: local(): full_recon = sum_by_axis_2(jnp.stack(stacked, axis=1), LAT, (2, 1, 0), 0)]
    all_to_all x2 -> x0, starting transfers between devices: 8.75 us -> none  [the longest x1 4.78 us: copy_for_each(): return lax.all_to_all(copies, axis, split_axis=0, concat_axis=0, tiled=True)]
  transfers between devices with their start and end apart: 4 -> 0, of which waited for: 4 -> 0; matrix products, arithmetic and copies ran while one was open for 2% -> 0% of each run, Pallas kernels for 0% -> 0%
where the time goes in v1:
time: 90.8 us; the launch traced here: 90.4 us
  Pallas kernels  81.8 us (90%)
  local copies, waits for them, and re-layouts  7.97 us (9%)
    pallas_call x1, Pallas kernels, local(): pl.pallas_call(functools.partial(kernel, sizes), out_shape=(jax.ShapeDtyp...  81.8 us
    unnamed x14, local copies, waits for them, and re-layouts  7.17 us

profile of v1, /device:TPU:1, one launch (start us, length us, event | category | flops | bytes accessed | tf_op | source)
XLA Modules:
  0.0 90.4 jit_solution(7486092170866582298)
XLA Ops:
  0.6 0.0 copy-start
  0.6 1.5 %copy-done = bf16[6,256,576]{1,2,0:T(8,128)(2,1)S(1)} copy-done((bf16[6,256,576]{1,2,0:T(8,128)(2,1)S(1)}, bf16[6,256,576]{1,2,0:T(8,128)(2,1)}, u32[]{:S(2)}) %copy-start) | copy-done | bytes 1769496
  2.1 0.0 copy-start.1
  2.1 1.2 %copy-done.1 = bf16[3,576,256]{2,1,0:T(8,128)(2,1)S(1)} copy-done((bf16[3,576,256]{2,1,0:T(8,128)(2,1)S(1)}, bf16[3,576,256]{2,1,0:T(8,128)(2,1)}, u32[]{:S(2)}) %copy-start.1) | copy-done | bytes 884760
  3.3 0.0 copy-start.2
  3.3 0.7 copy-done.2
  4.0 0.0 copy-start.3
  4.0 0.7 copy-done.3
  4.7 0.0 copy-start.4
  4.7 0.7 copy-done.4
  5.4 0.0 copy-start.5
  5.4 0.7 copy-done.5
  6.0 81.8 %shard_map.85 = (bf16[3,2,576]{2,1,0:T(2,128)(2,1)S(1)}, bf16[6,576,256]{2,1,0:T(8,128)(2,1)S(1)}, bf16[3,2,32,256]{3,2,1,0:T(8,128)(2,1)S(1)}) custom-call(bf16[3,2,576]{2,1,0:T(2,128)(2,1)S(1)} %bitcast.13, bf16[3,2,576]{2,1,0:T(2,128)(2,1)S(1)} %bitcast.14, bf16[3,576,256]{2,1,0:T(8,128)(2,1)S(1)} %copy-done.1, f32[3,256]{1,0:T(4,128)S(1)} %copy-done.4, ...), custom_call_target="tpu_custom_call" | custom-call | tf_op jit(solution)/shard_map/pallas_call | solution.py:288
  87.9 0.1 copy.9
  88.0 0.7 reshape.13
  88.6 0.6 copy.12
  89.2 1.2 %copy.13 = bf16[6,256,576]{1,2,0:T(8,128)(2,1)} copy(bf16[6,256,576]{1,2,0:T(8,128)(2,1)S(1)} %bitcast.12) | data formatting | bytes 3538944
  (1 shorter events, 0.0 us)
Async XLA Ops:
  0.6 1.5 %copy-start = (bf16[6,256,576]{1,2,0:T(8,128)(2,1)S(1)}, bf16[6,256,576]{1,2,0:T(8,128)(2,1)}, u32[]{:S(2)}) copy-start(bf16[6,256,576]{1,2,0:T(8,128)(2,1)} %param.10) | copy-start | bytes 5308420
  2.1 1.2 %copy-start.1 = (bf16[3,576,256]{2,1,0:T(8,128)(2,1)S(1)}, bf16[3,576,256]{2,1,0:T(8,128)(2,1)}, u32[]{:S(2)}) copy-start(bf16[3,576,256]{2,1,0:T(8,128)(2,1)} %ew_hbm.1) | copy-start | bytes 2654212
  3.3 0.7 copy-start.2
  4.0 0.7 copy-start.3
  4.7 0.7 copy-start.4
  5.4 0.7 copy-start.5

commit v2 on v1

v2 whole, which is shorter than its diff:
```python
import functools

import jax
import jax.numpy as jnp
from jax import lax
from jax.experimental import pallas as pl
from jax.experimental.pallas import tpu as pltpu
from jax.sharding import PartitionSpec as P

MESH = pl.DeviceIdType.MESH
F32 = jnp.float32
BF16 = jnp.bfloat16

CLASSES = 2

STEPS = {
    "a1": 15.0, "a2": 18.5, "a3": 19.5, "b1": 23.0, "b2": 26.0, "c1": 28.0,
    "c2": 31.5, "c3": 38.0, "d1": 43.5, "d2": 47.5, "d3": 48.5,
}
SPACING = 0.85


def block_index(source, target, layers):
    return source * layers - source * (source - 1) // 2 + (target - source)


def dot_nn(a, b):
    return lax.dot_general(a, b, (((1,), (0,)), ((), ())), preferred_element_type=F32)


def dot_nt(a, b):
    return lax.dot_general(a, b, (((1,), (1,)), ((), ())), preferred_element_type=F32)


def dot_tn(a, b):
    return lax.dot_general(a, b, (((0,), (0,)), ((), ())), preferred_element_type=F32)


def far_first(count):
    return sorted(range(1, count), key=lambda k: -min(k, count - k))


def kernel(
    sizes,
    in_hbm, tg_hbm, ew_hbm, bias_hbm, dw_hbm, cnt_hbm,
    recon_ref, dg_ref, lg_ref,
    own_in, tg, ew, bias, cnt, dw,
    zin, ga, pf, pp, pr, lt, rf, cr, ys, yr, zf, zs, zr, own_er, ez, ge, ef, es, er,
    load_sem, z_send, z_recv, y_send, y_recv, x_send, x_recv, c_send, c_recv,
):
    ny, nz, nx = sizes
    layers, pair, width = own_in.shape
    tile = ew.shape[2]
    classes = zin.shape[1]
    nq = nz // classes
    rows = nq * pair
    half = 2 * ny * rows
    lat = lax.axis_index("lat")
    x = lax.axis_index("tok")
    c = lax.rem(lat, 2)
    z = lax.rem(lax.div(lat, 2), nz)
    y = lax.div(lat, 2 * nz)
    mate = 1 - c
    zh = lax.rem(z, classes)
    zq = lax.div(z, classes)

    def device(y_at, z_at, c_at, x_at):
        return {"lat": (y_at * nz + z_at) * 2 + c_at, "tok": x_at}

    def z_peer(k):
        return device(y, k, c, x)

    def y_peer(k):
        return device(k, z, c, x)

    def x_peer(k):
        return device(y, z, c, k)

    core_peer = device(y, z, mate, x)

    barrier = pltpu.get_barrier_semaphore()
    for count, me, peer in ((nz, z, z_peer), (ny, y, y_peer), (nx, x, x_peer)):
        for k in far_first(count):
            pl.semaphore_signal(
                barrier, inc=1, device_id=peer(lax.rem(me + k, count)), device_id_type=MESH
            )
    pl.semaphore_signal(barrier, inc=1, device_id=core_peer, device_id_type=MESH)

    loads = [
        pltpu.make_async_copy(src, dst, load_sem.at[i])
        for i, (src, dst) in enumerate(
            ((in_hbm, own_in), (tg_hbm, tg), (bias_hbm, bias), (cnt_hbm, cnt), (ew_hbm, ew), (dw_hbm, dw))
        )
    ]
    for load in loads:
        load.start()
    loads[0].wait()
    pl.semaphore_wait(barrier, nz + ny + nx - 2)

    def send(src, dst, send_sem, recv_sem, to):
        pltpu.make_async_remote_copy(
            src_ref=src, dst_ref=dst, send_sem=send_sem, recv_sem=recv_sem, device_id=to, device_id_type=MESH
        ).start()

    def settle(ref, sem):
        pltpu.make_async_copy(ref, ref, sem).wait()

    def span(count):
        return pl.ds(0, count)

    every = range(layers)
    each = range(classes)
    chunks = [(l, h) for l in every for h in each]
    drains = []

    def z_gather(phase, l, h, own, slots):
        sends, recvs = z_send.at[phase, l, h], z_recv.at[phase, l, h]

        def start():
            @pl.when(zh == h)
            def _():
                @pl.loop(0, nz - 1)
                def _(k):
                    far = nz // 2 - lax.div(k + 1, 2)
                    to = lax.rem(z + nz + (1 - 2 * lax.rem(k + 1, 2)) * far, nz)
                    send(own.at[l], slots.at[l, h, zq], sends, recvs, z_peer(to))

        def arrive():
            @pl.when(zh != h)
            def _():
                settle(slots.at[l, h], recvs)

            if nq > 1:
                @pl.when(zh == h)
                def _():
                    settle(slots.at[l, h, span(nq - 1)], recvs)

        def drain():
            @pl.when(zh == h)
            def _():
                settle(zr.at[l, span(nz - 1)], sends)

        drains.append(drain)
        return start, arrive

    def z_scatter(m, h):
        sends, recvs = z_send.at[1, m, h], z_recv.at[1, m, 0]
        shift = lax.rem(h - zh + classes, classes)

        def one(step):
            to = lax.rem(z + shift + classes * step, nz)
            send(zs.at[m, h, lax.div(to, classes)], zr.at[m, z], sends, recvs, z_peer(to))

        def start():
            @pl.loop(0, nq - 1)
            def _(k):
                far = nq // 2 - lax.div(k + 1, 2)
                one(lax.rem(nq + (1 - 2 * lax.rem(k + 1, 2)) * far, nq))

            @pl.when(shift != 0)
            def _():
                one(0)

        def arrive():
            settle(zr.at[m, span(nz - 1)], recvs)

        def drain():
            @pl.when(shift != 0)
            def _():
                settle(zs.at[m, h], sends)

            if nq > 1:
                @pl.when(shift == 0)
                def _():
                    settle(zs.at[m, h, span(nq - 1)], sends)

        drains.append(drain)
        return start, arrive

    def exchange(count, me, peer, sends, recvs, part, slot, landed):
        def start():
            for k in far_first(count):
                to = lax.rem(me + k, count)
                send(part(to), slot(me), sends, recvs, peer(to))

        def arrive():
            settle(landed, recvs)

        def drain():
            settle(landed, sends)

        drains.append(drain)
        return start, arrive

    def y_exchange(phase, l, h, part, slot, landed):
        return exchange(
            ny, y, y_peer, y_send.at[phase, l, h], y_recv.at[phase, l, h], part, slot, landed
        )

    def x_exchange(phase, l, h, part, slot, landed):
        return exchange(
            nx, x, x_peer, x_send.at[phase, l, h], x_recv.at[phase, l, h], part, slot, landed
        )

    def swap(phase, l, h, src, dst, landing):
        sends, recvs = c_send.at[phase, l, h], c_recv.at[phase, l, h]
        drains.append(lambda: settle(landing, sends))
        return (lambda: send(src, dst, sends, recvs, core_peer)), (lambda: settle(landing, recvs))

    def table(make):
        return {(l, h): make(l, h) for l, h in chunks}

    a1 = table(lambda l, h: z_gather(0, l, h, own_in, zin))
    d1 = table(lambda l, h: z_gather(2, l, h, own_er, ez))
    c3 = table(z_scatter)

    def y_gather(phase, held):
        return table(
            lambda l, h: y_exchange(
                phase, l, h, lambda k: held.at[l, h, c, y], lambda k: held.at[l, h, c, k],
                held.at[l, h, c, span(ny - 1)],
            )
        )

    a2, d2 = y_gather(0, ga), y_gather(2, ge)
    c2 = table(
        lambda m, h: y_exchange(
            1, m, h, lambda k: ys.at[m, h, k], lambda k: yr.at[m, h, k], yr.at[m, h, span(ny - 1)]
        )
    )

    def x_scatter(phase, parts, slots):
        return table(
            lambda l, h: x_exchange(
                phase, l, h, lambda k: parts.at[l, h, :, k], lambda k: slots.at[l, h, k],
                slots.at[l, h, span(nx - 1)],
            )
        )

    b1, e1 = x_scatter(0, pp, pr), x_scatter(2, es, er)
    b2 = table(
        lambda l, h: x_exchange(
            1, l, h, lambda k: lt.at[l, h, :, x], lambda k: lt.at[l, h, :, k],
            lt.at[l, h, :, span(nx - 1)],
        )
    )
    a3 = table(lambda l, h: swap(0, l, h, ga.at[l, h, c], ga.at[l, h, c], ga.at[l, h, mate]))
    d3 = table(lambda l, h: swap(2, l, h, ge.at[l, h, c], ge.at[l, h, c], ge.at[l, h, mate]))
    c1 = table(lambda m, h: swap(1, m, h, rf.at[m, h, mate], cr.at[m, h], cr.at[m, h]))

    for chunk in chunks:
        a1[chunk][0]()
    for l in every:
        zin[l, zh, zq] = own_in[l]
    for load in loads[1:]:
        load.wait()

    def live(l):
        return lax.broadcasted_iota(jnp.int32, (1, tile), 1) < cnt[0:1, l : l + 1]

    def joined(blocks):
        return blocks.astype(F32).reshape(rows, width).astype(BF16)

    def step_a1(l, h):
        a1[l, h][1]()
        ga[l, h, c, y] = joined(zin[l, h])
        a2[l, h][0]()

    def step_a2(l, h):
        a2[l, h][1]()
        a3[l, h][0]()

    def step_a3(l, h):
        a3[l, h][1]()
        partial = dot_nn(ga[l, h].reshape(half, width), ew[l]).reshape(2, ny, rows, tile)
        pf[l, h] = partial
        pp[l, h] = partial.astype(BF16)
        b1[l, h][0]()

    def step_b1(l, h):
        b1[l, h][1]()
        summed = pf[l, h, :, x]
        for k in range(1, nx):
            summed = summed + pr[l, h, lax.rem(x + k, nx)].astype(F32)
        summed = summed + bias[l : l + 1, :].reshape(1, 1, tile)
        alive = live(l).reshape(1, 1, tile)
        lt[l, h, :, x] = jnp.where(alive, jnp.maximum(summed, 0.0), 0.0).astype(BF16)
        b2[l, h][0]()

    def step_b2(m, h):
        b2[m, h][1]()
        total = None
        for l in range(m + 1):
            term = dot_nt(lt[l, h].reshape(half, tile), dw[block_index(l, m, layers)])
            total = term if total is None else total + term
        rf[m, h] = total.reshape(2, ny, rows, width)
        c1[m, h][0]()

    def step_c1(m, h):
        c1[m, h][1]()
        ys[m, h] = (rf[m, h, c] + cr[m, h]).astype(BF16)
        c2[m, h][0]()

    def step_c2(m, h):
        c2[m, h][1]()
        summed = rf[m, h, c, y] + cr[m, h, y]
        for k in range(1, ny):
            summed = summed + yr[m, h, lax.rem(y + k, ny)].astype(F32)
        blocks = summed.reshape(nq, pair, width)
        zf[m, h] = blocks
        zs[m, h] = blocks.astype(BF16)
        c3[m, h][0]()

    def step_c3(m, h):
        @pl.when(zh == h)
        def _():
            c3[m, h][1]()
            full = zf[m, h, zq]
            for k in range(1, nz):
                full = full + zr[m, lax.rem(z + k, nz)].astype(F32)
            errors = (full - tg[m].astype(F32)).astype(BF16)
            own_er[m] = errors
            d1[m, h][0]()
            ez[m, h, zq] = errors
            recon_ref[m] = full.astype(BF16)

    def step_d1(m, h):
        d1[m, h][1]()
        ge[m, h, c, y] = joined(ez[m, h])
        d2[m, h][0]()

    def step_d2(m, h):
        d2[m, h][1]()
        d3[m, h][0]()

    def step_d3(m, h):
        d3[m, h][1]()
        rows_of = ge[m, h].reshape(half, width)
        for l in range(m + 1):
            term = dot_nn(rows_of, dw[block_index(l, m, layers)]).reshape(2, ny, rows, tile)
            term = term if l == m else ef[l, h] + term
            ef[l, h] = term
            if m == layers - 1:
                es[l, h] = term.astype(BF16)
                e1[l, h][0]()

    acts = dict(
        a1=step_a1, a2=step_a2, a3=step_a3, b1=step_b1, b2=step_b2, c1=step_c1,
        c2=step_c2, c3=step_c3, d1=step_d1, d2=step_d2, d3=step_d3,
    )
    order = sorted(
        (at + SPACING * i, name, chunk)
        for name, at in STEPS.items()
        for i, chunk in enumerate(chunks)
    )
    for _, name, chunk in order:
        acts[name](*chunk)

    for m in every:
        errors_of = ge[m].reshape(classes * half, width)
        for l in range(m + 1):
            latents_of = lt[l].reshape(classes * half, tile)
            dg_ref[block_index(l, m, layers)] = dot_tn(errors_of, latents_of).astype(BF16)
    late = [(l, h) for h in each for l in every]
    for drain in drains:
        drain()
    for l, h in late:
        e1[l, h][1]()
        summed = ef[l, h, :, x]
        for k in range(1, nx):
            summed = summed + er[l, h, lax.rem(x + k, nx)].astype(F32)
        summed = jnp.where(live(l).reshape(1, 1, tile), summed, 0.0)
        pf[l, h, :, 0] = summed
    for l in every:
        by_owner = pf[l, :, :, 0].reshape(classes, 2, nq, pair, tile).transpose(2, 0, 1, 3, 4)
        lg_ref[l] = by_owner.reshape(classes * 2 * rows, tile).astype(BF16)


def store(a_ref, b_ref, c_ref, a_out, b_out, c_out, sem):
    copies = [
        pltpu.make_async_copy(src, dst, sem.at[i])
        for i, (src, dst) in enumerate(((a_ref, a_out), (b_ref, b_out), (c_ref, c_out)))
    ]
    for copy in copies:
        copy.start()
    for copy in copies:
        copy.wait()


def build(mesh, sizes, classes):
    ny, nz, nx = sizes

    def local(inputs, targets, enc_weight, enc_bias, dec_weight, counts):
        pair, layers, width = inputs.shape
        tile = enc_weight.shape[2]
        blocks = dec_weight.shape[0]
        nq = nz // classes
        rows = nq * pair
        lh = (layers, classes)
        in_hbm = pl.BlockSpec(memory_space=pltpu.HBM)
        in_vmem = pl.BlockSpec(memory_space=pltpu.VMEM)

        def vmem(*shape, dtype=BF16):
            return pltpu.VMEM(shape, dtype)

        def sems(*shape):
            return pltpu.SemaphoreType.DMA(shape)

        operands = (
            inputs.transpose(1, 0, 2),
            targets.transpose(1, 0, 2),
            enc_weight,
            enc_bias,
            dec_weight.transpose(0, 2, 1),
            counts.T,
        )
        computed = pl.pallas_call(
            functools.partial(kernel, sizes),
            out_shape=(
                pltpu.VMEM((layers, pair, width), BF16),
                pltpu.VMEM((blocks, width, tile), BF16),
                pltpu.VMEM((layers, classes * 2 * rows, tile), BF16),
            ),
            in_specs=[in_hbm] * 6,
            out_specs=(in_vmem, in_vmem, in_vmem),
            scratch_shapes=[
                vmem(layers, pair, width),
                vmem(layers, pair, width),
                vmem(layers, width, tile),
                vmem(layers, tile, dtype=F32),
                vmem(1, layers, dtype=jnp.int32),
                vmem(blocks, width, tile),
                vmem(*lh, nq, pair, width),
                vmem(*lh, 2, ny, rows, width),
                vmem(*lh, 2, ny, rows, tile, dtype=F32),
                vmem(*lh, 2, ny, rows, tile),
                vmem(*lh, nx, 2, rows, tile),
                vmem(*lh, 2, ny, rows, tile),
                vmem(*lh, 2, ny, rows, width, dtype=F32),
                vmem(*lh, ny, rows, width, dtype=F32),
                vmem(*lh, ny, rows, width),
                vmem(*lh, ny, rows, width),
                vmem(*lh, nq, pair, width, dtype=F32),
                vmem(*lh, nq, pair, width),
                vmem(layers, nz, pair, width),
                vmem(layers, pair, width),
                vmem(*lh, nq, pair, width),
                vmem(*lh, 2, ny, rows, width),
                vmem(*lh, 2, ny, rows, tile, dtype=F32),
                vmem(*lh, 2, ny, rows, tile),
                vmem(*lh, nx, 2, rows, tile),
                sems(6),
                *(sems(3, *lh) for _ in range(8)),
            ],
            compiler_params=pltpu.CompilerParams(
                collective_id=0, has_side_effects=True, vmem_limit_bytes=48 * 1024 * 1024
            ),
        )(*(pltpu.with_memory_space_constraint(array, pltpu.HBM) for array in operands))
        recon, dec_grad, latent_grad = pl.pallas_call(
            store,
            out_shape=tuple(pltpu.HBM(part.shape, part.dtype) for part in computed),
            in_specs=[in_vmem] * 3,
            out_specs=(in_hbm,) * 3,
            scratch_shapes=[sems(3)],
            compiler_params=pltpu.CompilerParams(vmem_limit_bytes=1024 * 1024),
        )(*computed)
        return (
            recon.transpose(1, 0, 2),
            dec_grad.transpose(0, 2, 1),
            latent_grad.transpose(1, 0, 2),
        )

    in_specs = (
        P("lat", None, "tok"),
        P("lat", None, "tok"),
        P(None, "tok", "lat"),
        P(None, "lat"),
        P(None, "lat", "tok"),
        P(None, "lat"),
    )
    out_specs = (P("lat", None, "tok"), P(None, "lat", "tok"), P("tok", None, "lat"))
    return jax.shard_map(local, mesh=mesh, in_specs=in_specs, out_specs=out_specs, check_vma=False)


def solution(mesh):
    nx = mesh.shape["tok"]
    return build(mesh, (4, mesh.shape["lat"] // 8, nx), CLASSES)
```

time: 90.8 us -> 75.7 us (0.83)
  local copies, waits for them, and re-layouts: 7.97 us -> 0 us
  Pallas kernels: 81.8 us -> 75 us
    unnamed x14 -> x0, local copies, waits for them, and re-layouts: 7.17 us -> none
    pallas_call x1 -> x2, Pallas kernels: 81.8 us -> 75 us  [the longest x1 73.7 us: local(): pl.pallas_call(functools.partial(kernel, sizes), out_shape=(pltpu.VMEM((l...]
where the time goes in v2:
time: 75.7 us; the launch traced here: 75.6 us
  Pallas kernels  75 us (99%)
    pallas_call x1, Pallas kernels, local(): pl.pallas_call(functools.partial(kernel, sizes), out_shape=(pltpu.VMEM((l...  73.7 us

profile of v2, /device:TPU:1, one launch (start us, length us, event | category | flops | bytes accessed | tf_op | source)
XLA Modules:
  0.0 75.6 jit_solution(9833596738406642568)
XLA Ops:
  0.6 73.7 %shard_map.85 = (bf16[3,2,576]{2,1,0:T(2,128)(2,1)S(1)}, bf16[6,576,256]{2,1,0:T(8,128)(2,1)S(1)}, bf16[3,64,256]{2,1,0:T(8,128)(2,1)S(1)}) custom-call(bf16[3,2,576]{2,1,0:T(2,128)(2,1)} %bitcast.8, bf16[3,2,576]{2,1,0:T(2,128)(2,1)} %bitcast.9, bf16[3,576,256]{2,1,0:T(8,128)(2,1)} %ew_hbm.1, f32[3,256]{1,0:T(4,128)} %bias_hbm.1, ...), custom_call_target="tpu_custom_call" | custom-call | tf_op jit(solution)/shard_map/pallas_call | solution.py:417
  74.3 1.3 %shard_map.86 = (bf16[3,2,576]{2,1,0:T(2,128)(2,1)}, bf16[6,576,256]{2,1,0:T(8,128)(2,1)}, bf16[3,64,256]{2,1,0:T(8,128)(2,1)}) custom-call(bf16[3,2,576]{2,1,0:T(2,128)(2,1)S(1)} %get-tuple-element.9.a_ref, bf16[6,576,256]{2,1,0:T(8,128)(2,1)S(1)} %get-tuple-element.10.b_ref, bf16[3,64,256]{2,1,0:T(8,128)(2,1)S(1)} %get-tuple-element.11.c_ref), custom_call_target="tpu_custom_call" | custom-call | tf_op jit(solution)/shard_map/pallas_call | solution.py:459
